TPU v7x, 128 devices: a whole 4x4x4 slice. The times are simulated.
128 devices in a mesh: img: 16 (over y, z), pix: 8 (over x, core).
Axes of the slice: x: 4, y: 4, z: 4, core: 2. Of those that a mesh axis runs over, the one named last changes fastest.
Arguments:
- images: bfloat16 [6144, 16384], P('img', 'pix'), may hold values from -12 to 12
- inverse_noise_scale: float32 [6144], P('img'), may hold values from 0.4 to 4
- projections: bfloat16 [16384, 16384], P('img', 'pix'), may hold values from -1 to 1
- group_search_blocks: int32 [16, 16], P('img'), may hold values from 0 to 127, as said below
- search_list_count: int32 [16], P('img'), may hold values from 12 to 16, as said below
Outputs:
- projection_sums: float32 [16384, 16384], P('img', 'pix')
- log_evidence: float32 [6144], P(('img', 'pix'))
Inputs may be any that keep to these rules, and one draw needn't show every extreme that they name: `group_search_blocks`: each row lists 16 different block ids; block b is owned by index b // 8 of img. Among the first search_list_count[g] entries of row g no owner appears more than 2 times, and in every draw one owner has 2 of its blocks among the first 2 entries of every row. `search_list_count`: some group's count is 16 in every draw.
All inputs are finite; a program needn't handle non-finite values.
Results may differ from a plain program's by a relative error of at most 0.004.
Values may be sent and summed in bfloat16 or wider, within the bound.
A program may use at most 128 MiB of HBM per device.

v0:
```python
import jax
import jax.numpy as jnp
from jax import lax
from jax.sharding import PartitionSpec as P

BLOCK = 128
CAP = 2
MAXL = 16


def on_device(images, inverse_noise_scale, projections, group_search_blocks, search_list_count):
    group_rows, pixels = images.shape
    n_groups = lax.axis_size("img")
    n_shares = lax.axis_size("pix")
    share_rows = group_rows // n_shares
    owned_blocks = projections.shape[0] // BLOCK
    own_index = lax.axis_index("img")
    first_row = lax.axis_index("pix") * share_rows
    everyone = lax.all_gather(images, "img", axis=0, tiled=True).reshape(
        n_groups, group_rows, pixels
    )
    small = jnp.concatenate(
        [
            group_search_blocks.astype(jnp.float32),
            search_list_count[:, None].astype(jnp.float32),
            lax.dynamic_slice_in_dim(inverse_noise_scale, first_row, share_rows)[None],
        ],
        axis=1,
    )
    table = lax.all_gather(small, "img", axis=0, tiled=True)
    every_list = table[:, :MAXL].astype(jnp.int32)
    every_count = table[:, MAXL].astype(jnp.int32)
    scaling = table[:, MAXL + 1 :]
    positions = jnp.arange(MAXL, dtype=jnp.int32)
    slot_ids = jnp.arange(CAP, dtype=jnp.int32)
    live_entry = positions[None, :] < every_count[:, None]
    local_hit = live_entry & (every_list // owned_blocks == own_index)
    slot_rank = jnp.cumsum(local_hit.astype(jnp.int32), axis=1) - 1
    slot_pick = local_hit[:, None, :] & (slot_rank[:, None, :] == slot_ids[None, :, None])
    slot_offset = jnp.sum(jnp.where(slot_pick, every_list[:, None, :] % owned_blocks, 0), axis=2)
    slot_filled = jnp.any(slot_pick, axis=2)
    stacked = projections.reshape(owned_blocks, BLOCK, pixels)
    outgoing = jnp.take(stacked, slot_offset.reshape(-1), axis=0).reshape(
        n_groups, CAP * BLOCK, pixels
    )
    local_scores = jnp.einsum(
        "gif,gsf->gis", everyone, outgoing, preferred_element_type=jnp.float32
    )
    scores = lax.psum_scatter(local_scores, "pix", scatter_dimension=1, tiled=True)
    live = jnp.repeat(slot_filled, BLOCK, axis=1)[:, None, :]
    logits = jnp.where(live, scores * scaling[:, :, None], jnp.float32(-1e30))
    peak = jnp.max(logits, axis=2)
    total = jnp.sum(jnp.where(live, jnp.exp(logits - peak[:, :, None]), 0.0), axis=2)
    stats = lax.all_gather(jnp.stack([peak, total]), "img", axis=0)
    row_peak = jnp.max(stats[:, 0], axis=0)
    row_total = jnp.sum(stats[:, 1] * jnp.exp(stats[:, 0] - row_peak[None]), axis=0)
    evidence = row_peak + jnp.log(row_total)
    evidence_out = lax.dynamic_index_in_dim(evidence, own_index, 0, keepdims=False)
    exponent = jnp.where(live, jnp.exp(logits - row_peak[:, :, None]), 0.0)
    weights = (exponent / row_total[:, :, None]).astype(jnp.bfloat16)
    weights = lax.all_gather(weights, "pix", axis=1, tiled=True)
    arriving = jnp.einsum(
        "gis,gif->gsf", weights, everyone, preferred_element_type=jnp.float32
    ).astype(jnp.bfloat16)
    placement = (
        slot_offset.reshape(-1)[None, :] == jnp.arange(owned_blocks, dtype=jnp.int32)[:, None]
    ) & slot_filled.reshape(-1)[None, :]
    running_total = jnp.dot(
        placement.astype(jnp.bfloat16),
        arriving.reshape(n_groups * CAP, BLOCK * pixels),
        preferred_element_type=jnp.float32,
    )
    return (running_total.reshape(owned_blocks * BLOCK, pixels), evidence_out)


def solution(mesh):
    placed = (P("img", "pix"), P("img"), P("img", "pix"), P("img", None), P("img"))
    return jax.shard_map(
        on_device,
        mesh=mesh,
        in_specs=placed,
        out_specs=(P("img", "pix"), P(("img", "pix"))),
        check_vma=False,
    )
```

profile of v0, /device:TPU:1, one launch (start us, length us, event | category | flops | bytes accessed | tf_op | source)
XLA Modules:
  0.0 353.3 jit_solution(5376012222658015447)
XLA Ops:
  7.2 0.0 copy-start
  7.2 0.0 all-gather.5.cloned.1.call-start
  7.2 0.7 all-gather.5.cloned.1.call-update
  7.9 0.0 reduce-scatter.2.cloned.1.call-start
  8.6 0.7 convert_element_type.26
  9.3 0.0 copy-done
  9.3 0.1 dynamic-slice_bitcast_fusion
  9.3 0.1 maximum_bitcast_fusion
  9.4 18.4 %all-gather.1 = f32[16,1,65]{2,1,0:T(1,128)S(1)} all-gather(f32[1,1,65]{2,1,0:T(1,128)S(1)} %maximum_bitcast_fusion), channel_id=1, replica_groups=mesh['img'=16,'pix'=8] {'img'}, dimensions={0}, use_global_device_ids=true | all-gather | bytes 4420 | tf_op jit(solution)/shard_map/all_gather | solution.py:30
  27.8 0.2 fusion.8
  28.0 0.1 fusion.20
  28.1 0.2 reduce_window_sum.11
  28.3 0.1 select_reduce_fusion.1
  28.4 0.1 copy.35
  28.5 0.1 reshape.83
  28.6 0.1 copy.38
  28.7 0.1 broadcast_in_dim.79
  28.8 9.3 %gather_fusion = bf16[32,128,2048]{2,1,0:T(8,128)(2,1)} fusion(bf16[8,128,2048]{2,1,0:T(8,128)(2,1)} %bitcast.48, s32[1024]{0:T(1024)S(1)} %pad_clamp_fusion), kind=kCustom, calls=%fused_computation | custom fusion | bytes 33554560 | tf_op jit(solution)/shard_map/jit(_take)/gather | solution.py:43
  38.1 14.3 %bitcast_select_fusion = bf16[16,256,2048]{2,1,0:T(8,128)(2,1)} fusion(pred[16,256]{1,0:T(8,128)(4,1)S(1)} %bitcast.64, bf16[16,256,2048]{2,1,0:T(8,128)(2,1)} %bitcast.47), kind=kLoop, calls=%fused_computation.1 | loop fusion | flops 8388608 | bytes 33558528 | tf_op jit(solution)/shard_map/jit(_take)/select_n | solution.py:43
  52.4 115.0 %all-gather.5.cloned.1.call-done = bf16[6144,2048]{1,0:T(8,128)(2,1)} async-done(((bf16[384,2048]{1,0:T(8,128)(2,1)}), bf16[6144,2048]{1,0:T(8,128)(2,1)}) %all-gather.5.cloned.1.call-update) | async-done | bytes 25165840 | tf_op jit(solution)/shard_map/all_gather | solution.py:19
  167.5 18.7 %convolution_bitcast_fusion = f32[16,384,256]{1,2,0:T(8,128)} fusion(bf16[16,256,2048]{2,1,0:T(8,128)(2,1)} %bitcast_select_fusion, bf16[16,384,2048]{2,1,0:T(8,128)(2,1)} %bitcast.49), kind=kOutput, calls=%fused_computation.4 | convolution fusion | flops 6442450944 | bytes 48234496 | tf_op jit(solution)/shard_map/gif,gsf->gis/dot_general | solution.py:46
  186.2 6.7 %copy.40 = f32[16,384,256]{2,0,1:T(8,128)} copy(f32[16,384,256]{1,2,0:T(8,128)} %convolution_bitcast_fusion) | data formatting | bytes 12582912 | tf_op jit(solution)/shard_map/gif,gsf->gis/dot_general | solution.py:46
  192.9 0.0 reduce-scatter.2.cloned.1.call-update
  192.9 0.0 all-gather.7.cloned.1.call-start
  193.0 0.1 slice.25
  193.0 0.1 fusion.6
  193.1 0.1 copy.36
  193.3 0.1 broadcast_in_dim.76
  193.4 0.1 copy.41
  193.4 41.3 %reduce-scatter.2.cloned.1.call-done = f32[16,48,256]{2,0,1:T(8,128)} async-done(((f32[16,384,256]{2,0,1:T(8,128)}), f32[16,48,256]{2,0,1:T(8,128)}) %reduce-scatter.2.cloned.1.call-update) | async-done | bytes 786448 | tf_op jit(solution)/shard_map/reduce_scatter | solution.py:49
  234.7 1.4 fusion.1
  236.2 1.5 select_reduce_fusion
  237.7 0.1 copy.43
  237.8 0.1 copy.42
  237.8 18.9 %all-gather = f32[32,16,48]{2,1,0:T(8,128)S(1)} all-gather(f32[2,16,48]{2,1,0:T(8,128)S(1)} %pad_maximum_fusion), channel_id=2, replica_groups=mesh['img'=16,'pix'=8] {'img'}, dimensions={0}, use_global_device_ids=true | all-gather | bytes 104448 | tf_op jit(solution)/shard_map/all_gather | solution.py:54
  256.8 0.1 copy.45
  256.9 0.1 copy.46
  257.0 2.3 divide_convert_fusion
  259.3 0.0 all-gather.7.cloned.1.call-update
  259.3 0.1 and.47
  259.4 0.1 eq.41
  259.5 0.5 fusion.19
  260.0 30.4 %all-gather.7.cloned.1.call-done = bf16[16,384,256]{2,0,1:T(8,128)(2,1)} async-done(((bf16[16,48,256]{2,0,1:T(8,128)(2,1)}), bf16[16,384,256]{2,0,1:T(8,128)(2,1)}) %all-gather.7.cloned.1.call-update) | async-done | bytes 3145744 | tf_op jit(solution)/shard_map/all_gather | solution.py:61
  290.4 21.9 %convolution_convert_fusion = bf16[16,256,2048]{2,1,0:T(8,128)(2,1)} fusion(bf16[16,384,2048]{2,1,0:T(8,128)(2,1)} %bitcast.50, bf16[16,384,256]{2,0,1:T(8,128)(2,1)} %all-gather.7.cloned.1.call-done), kind=kOutput, calls=%fused_computation.2 | convolution fusion | flops 6450839552 | bytes 45088768 | tf_op jit(solution)/shard_map/gis,gif->gsf/dot_general | solution.py:62
  312.3 14.9 %reshape.85 = bf16[32,262144]{1,0:T(8,128)(2,1)} reshape(bf16[16,256,2048]{2,1,0:T(8,128)(2,1)} %convolution_convert_fusion) | data formatting | bytes 33554432 | tf_op jit(solution)/shard_map/reshape | solution.py:70
  327.2 11.3 %fusion.14 = f32[8,262144]{1,0:T(8,128)} fusion(bf16[32,262144]{1,0:T(8,128)(2,1)} %reshape.85, s32[32]{0:T(128)S(1)} %eq.41, pred[32]{0:T(512)(128)(4,1)S(1)} %and.47), kind=kOutput, calls=%fused_computation.41 | convolution fusion | flops 134218240 | bytes 25165984 | tf_op jit(solution)/shard_map/dot_general | solution.py:68
  338.5 8.3 %reshape.86 = f32[1024,2048]{1,0:T(8,128)} reshape(f32[8,262144]{1,0:T(8,128)} %fusion.14) | data formatting | bytes 16777216 | tf_op jit(solution)/shard_map/reshape | solution.py:73
  346.8 0.0 copy-done.1
  (10 shorter events, 0.1 us)
Async XLA Ops:
  7.2 2.1 copy-start
  7.2 160.3 %all-gather.5.cloned.1.call-start = ((), (), s32[]{:S(2)}) async-start(), calls=%async_computation.1 | async-start | bytes 26738688 | tf_op jit(solution)/shard_map/all_gather | solution.py:19
  7.9 226.8 %reduce-scatter.2.cloned.1.call-start = ((), (), s32[]{:S(2)}) async-start(), calls=%async_computation.2 | async-start | bytes 7077888 | tf_op jit(solution)/shard_map/reduce_scatter | solution.py:49
  192.9 97.5 %all-gather.7.cloned.1.call-start = ((), (), s32[]{:S(2)}) async-start(), calls=%async_computation.3 | async-start | bytes 3538944 | tf_op jit(solution)/shard_map/all_gather | solution.py:61
  312.3 34.5 %copy-start.1 = (f32[384]{0:T(512)S(1)}, f32[384]{0:T(512)}, u32[]{:S(2)}) copy-start(f32[384]{0:T(512)} %param.6) | copy-start | bytes 4612
Sparse Core Ops, SparseCore 0:
  10.2 157.2 all-gather.4
  193.0 41.6 reduce-scatter.1
  259.4 30.9 all-gather.6
where the time goes:
time: 354 us; the launch traced here: 353 us
  waiting for transfers between devices  187 us (53%)
  matrix products  51.9 us (15%)
  local copies, waits for them, and re-layouts  40.5 us (11%)
  blocking collectives  37.3 us (11%)
  other arithmetic  21.5 us (6%)
  between operations  14.5 us (4%)
    all_gather x1, waiting for transfers between devices, on_device(): lax.all_gather(images, 'img', axis=0, tiled=True)  115 us
    reduce_scatter x1, waiting for transfers between devices, on_device(): lax.psum_scatter(local_scores, 'pix', scatter_dimension=1, tiled=True)  41.3 us
    all_gather x1, waiting for transfers between devices, on_device(): weights = lax.all_gather(weights, 'pix', axis=1, tiled=True)  30.4 us
    dot_general x1, matrix products, on_device(): jnp.einsum('gis,gif->gsf', weights, everyone, preferred_element_type=jnp....  21.9 us
    all_gather x1, blocking collectives, on_device(): stats = lax.all_gather(jnp.stack([peak, total]), 'img', axis=0)  18.9 us
    dot_general x1, matrix products, on_device(): jnp.einsum('gif,gsf->gis', everyone, outgoing, preferred_element_type=jnp...  18.7 us
    all_gather x1, blocking collectives, on_device(): table = lax.all_gather(small, 'img', axis=0, tiled=True)  18.4 us
    reshape x1, local copies, waits for them, and re-layouts, on_device(): arriving.reshape(n_groups * CAP, BLOCK * pixels)  14.9 us
  transfers between devices with their start and end apart: 3, of which 3 were waited for; matrix products, arithmetic and copies ran while one was open for 8% of the time, Pallas kernels for 0%

commit v1 on v0

--- a/solution.py
+++ b/solution.py
@@ -1,3 +1,4 @@
+import functools
 import jax
 import jax.numpy as jnp
 from jax import lax
@@ -8,6 +9,22 @@
 MAXL = 16
 
 
+def recast_columns(mine_x, chip_axis):
+    passed = jnp.concatenate(
+        lax.all_to_all(
+            jnp.stack([mine_x for _ in range(lax.axis_size(chip_axis))], 0),
+            axis_name=chip_axis,
+            split_axis=0,
+            concat_axis=0,
+        ),
+        0,
+    )
+    return passed
+
+
+check_sections_by_axis = functools.partial(recast_columns, chip_axis="img")
+
+
 def on_device(images, inverse_noise_scale, projections, group_search_blocks, search_list_count):
     group_rows, pixels = images.shape
     n_groups = lax.axis_size("img")
@@ -16,9 +33,7 @@
     owned_blocks = projections.shape[0] // BLOCK
     own_index = lax.axis_index("img")
     first_row = lax.axis_index("pix") * share_rows
-    everyone = lax.all_gather(images, "img", axis=0, tiled=True).reshape(
-        n_groups, group_rows, pixels
-    )
+    everyone = check_sections_by_axis(images).reshape(n_groups, group_rows, pixels)
     small = jnp.concatenate(
         [
             group_search_blocks.astype(jnp.float32),

time: 354 us -> 710 us (2.01)
  blocking collectives: 37.3 us -> 486 us
  waiting for transfers between devices: 187 us -> 77.6 us
  local copies, waits for them, and re-layouts: 40.5 us -> 50.1 us
  starting transfers between devices: 0.12 us -> 8.85 us
    all_gather x1, blocking collectives: 18.4 us -> 467 us  [on_device(): table = lax.all_gather(small, 'img', axis=0, tiled=True)]
    all_gather x1 -> x0, waiting for transfers between devices: 115 us -> none  [on_device(): lax.all_gather(images, 'img', axis=0, tiled=True)]
    another operation x0 -> x1, local copies, waits for them, and re-layouts: none -> 9.57 us  [recast_columns(): jnp.stack([mine_x for _ in range(lax.axis_size(chip_axis))], 0)]
    all_to_all x0 -> x1, starting transfers between devices: none -> 8.76 us  [recast_columns(): lax.all_to_all(jnp.stack([mine_x for _ in range(lax.axis_size(chip_axis))...]
  transfers between devices with their start and end apart: 3 -> 3, of which waited for: 3 -> 2; matrix products, arithmetic and copies ran while one was open for 8% -> 4% of each run, Pallas kernels for 0% -> 0%
where the time goes in v1:
time: 710 us
  blocking collectives  486 us (68%)
  waiting for transfers between devices  77.6 us (11%)
  matrix products  51.9 us (7%)
  local copies, waits for them, and re-layouts  50.1 us (7%)
  other arithmetic  20.8 us (3%)
  between operations  14.8 us (2%)
  starting transfers between devices  8.85 us (1%)
    all_gather x1, blocking collectives, on_device(): table = lax.all_gather(small, 'img', axis=0, tiled=True)  467 us
    reduce_scatter x1, waiting for transfers between devices, on_device(): lax.psum_scatter(local_scores, 'pix', scatter_dimension=1, tiled=True)  47.1 us
    all_gather x1, waiting for transfers between devices, on_device(): weights = lax.all_gather(weights, 'pix', axis=1, tiled=True)  30.4 us
    dot_general x1, matrix products, on_device(): jnp.einsum('gis,gif->gsf', weights, everyone, preferred_element_type=jnp....  21.9 us
    all_gather x1, blocking collectives, on_device(): stats = lax.all_gather(jnp.stack([peak, total]), 'img', axis=0)  18.9 us
    dot_general x1, matrix products, on_device(): jnp.einsum('gif,gsf->gis', everyone, outgoing, preferred_element_type=jnp...  18.7 us
    reshape x1, local copies, waits for them, and re-layouts, on_device(): arriving.reshape(n_groups * CAP, BLOCK * pixels)  14.9 us
  transfers between devices with their start and end apart: 3, of which 2 were waited for; matrix products, arithmetic and copies ran while one was open for 4% of the time, Pallas kernels for 0%

profile of v1, /device:TPU:1, one launch (start us, length us, event | category | flops | bytes accessed | tf_op | source)
XLA Modules:
  0.0 709.6 jit_solution(13240052928875503686)
XLA Ops:
  7.2 0.0 copy-start
  7.2 9.6 %stack.8 = bf16[16,384,2048]{2,1,0:T(8,128)(2,1)} broadcast(bf16[384,2048]{1,0:T(8,128)(2,1)} %param.5), dimensions={1,2} | broadcast | bytes 26738688 | tf_op jit(solution)/shard_map/stack | solution.py:15
  16.8 8.8 %all-to-all-start = ((bf16[16,384,2048]{2,1,0:T(8,128)(2,1)}), bf16[16,384,2048]{2,1,0:T(8,128)(2,1)}, u32[]{:S(2)}, u32[]{:S(2)}) async-start(bf16[16,384,2048]{2,1,0:T(8,128)(2,1)} %stack.8), calls=%async_computation | async-start | bytes 50331648 | tf_op jit(solution)/shard_map/all_to_all | solution.py:14
  25.5 0.0 reduce-scatter.2.cloned.1.call-start
  26.2 0.0 copy-done.2
  26.2 0.0 copy-done
  26.3 0.1 dynamic-slice_bitcast_fusion
  26.3 0.1 maximum_bitcast_fusion
  26.4 466.7 %all-gather.1 = f32[16,1,65]{2,1,0:T(1,128)S(1)} all-gather(f32[1,1,65]{2,1,0:T(1,128)S(1)} %maximum_bitcast_fusion), channel_id=1, replica_groups=mesh['img'=16,'pix'=8] {'img'}, dimensions={0}, use_global_device_ids=true | all-gather | bytes 4420 | tf_op jit(solution)/shard_map/all_gather | solution.py:45
  493.1 0.2 fusion.8
  493.3 0.1 fusion.20
  493.4 0.2 reduce_window_sum.11
  493.6 0.1 select_reduce_fusion.1
  493.7 0.1 copy.35
  493.8 0.1 copy.38
  493.9 0.1 broadcast_in_dim.79
  494.0 0.1 reshape.82
  494.1 9.3 %gather_fusion = bf16[32,128,2048]{2,1,0:T(8,128)(2,1)} fusion(bf16[8,128,2048]{2,1,0:T(8,128)(2,1)} %bitcast.47, s32[1024]{0:T(1024)S(1)} %pad_clamp_fusion), kind=kCustom, calls=%fused_computation | custom fusion | bytes 33554560 | tf_op jit(solution)/shard_map/jit(_take)/gather | solution.py:58
  503.5 14.2 %bitcast_select_fusion = bf16[16,256,2048]{2,1,0:T(8,128)(2,1)} fusion(pred[16,256]{1,0:T(8,128)(4,1)S(1)} %bitcast.61, bf16[16,256,2048]{2,1,0:T(8,128)(2,1)} %bitcast.46), kind=kLoop, calls=%fused_computation.1 | loop fusion | flops 8388608 | bytes 33558528 | tf_op jit(solution)/shard_map/jit(_take)/select_n | solution.py:58
  517.6 0.0 all-to-all-done
  517.6 18.7 %convolution_bitcast_fusion = f32[16,384,256]{1,2,0:T(8,128)} fusion(bf16[16,256,2048]{2,1,0:T(8,128)(2,1)} %bitcast_select_fusion, bf16[16,384,2048]{2,1,0:T(8,128)(2,1)} %all-to-all-done), kind=kOutput, calls=%fused_computation.4 | convolution fusion | flops 6442450944 | bytes 48234496 | tf_op jit(solution)/shard_map/gif,gsf->gis/dot_general | solution.py:61
  536.4 6.7 copy.40
  543.0 0.0 reduce-scatter.2.cloned.1.call-update
  543.1 0.0 all-gather.4.cloned.1.call-start
  543.1 0.1 slice.25
  543.2 0.1 copy.41
  543.3 0.1 fusion.6
  543.4 0.1 copy.36
  543.5 0.1 broadcast_in_dim.76
  543.6 47.1 %reduce-scatter.2.cloned.1.call-done = f32[16,48,256]{2,0,1:T(8,128)} async-done(((f32[16,384,256]{2,0,1:T(8,128)}), f32[16,48,256]{2,0,1:T(8,128)}) %reduce-scatter.2.cloned.1.call-update) | async-done | bytes 786448 | tf_op jit(solution)/shard_map/reduce_scatter | solution.py:64
  590.7 1.4 fusion.1
  592.2 1.5 select_reduce_fusion
  593.7 0.1 copy.43
  593.8 0.1 copy.42
  593.8 18.9 %all-gather = f32[32,16,48]{2,1,0:T(8,128)S(1)} all-gather(f32[2,16,48]{2,1,0:T(8,128)S(1)} %pad_maximum_fusion), channel_id=2, replica_groups=mesh['img'=16,'pix'=8] {'img'}, dimensions={0}, use_global_device_ids=true | all-gather | bytes 104448 | tf_op jit(solution)/shard_map/all_gather | solution.py:69
  612.8 0.1 copy.45
  612.9 0.1 copy.46
  613.0 2.3 divide_convert_fusion
  615.3 0.0 all-gather.4.cloned.1.call-update
  615.3 0.1 eq.41
  615.4 0.1 and.47
  615.5 0.5 fusion.19
  616.0 30.4 %all-gather.4.cloned.1.call-done = bf16[16,384,256]{2,0,1:T(8,128)(2,1)} async-done(((bf16[16,48,256]{2,0,1:T(8,128)(2,1)}), bf16[16,384,256]{2,0,1:T(8,128)(2,1)}) %all-gather.4.cloned.1.call-update) | async-done | bytes 3145744 | tf_op jit(solution)/shard_map/all_gather | solution.py:76
  646.4 21.9 %convolution_convert_fusion = bf16[16,256,2048]{2,1,0:T(8,128)(2,1)} fusion(bf16[16,384,2048]{2,1,0:T(8,128)(2,1)} %all-to-all-done, bf16[16,384,256]{2,0,1:T(8,128)(2,1)} %all-gather.4.cloned.1.call-done), kind=kOutput, calls=%fused_computation.2 | convolution fusion | flops 6450839552 | bytes 45088768 | tf_op jit(solution)/shard_map/gis,gif->gsf/dot_general | solution.py:77
  668.3 14.9 %reshape.83 = bf16[32,262144]{1,0:T(8,128)(2,1)} reshape(bf16[16,256,2048]{2,1,0:T(8,128)(2,1)} %convolution_convert_fusion) | data formatting | bytes 33554432 | tf_op jit(solution)/shard_map/reshape | solution.py:85
  683.2 11.3 %fusion.14 = f32[8,262144]{1,0:T(8,128)} fusion(bf16[32,262144]{1,0:T(8,128)(2,1)} %reshape.83, s32[32]{0:T(128)S(1)} %eq.41, pred[32]{0:T(512)(128)(4,1)S(1)} %and.47), kind=kOutput, calls=%fused_computation.41 | convolution fusion | flops 134218240 | bytes 25165984 | tf_op jit(solution)/shard_map/dot_general | solution.py:83
  694.5 8.3 %reshape.84 = f32[1024,2048]{1,0:T(8,128)} reshape(f32[8,262144]{1,0:T(8,128)} %fusion.14) | data formatting | bytes 16777216 | tf_op jit(solution)/shard_map/reshape | solution.py:88
  702.8 0.0 copy-done.1
  (12 shorter events, 0.1 us)
Async XLA Ops:
  7.2 19.1 %copy-start = (f32[384]{0:T(512)S(1)}, f32[384]{0:T(512)}, u32[]{:S(2)}) copy-start(f32[384]{0:T(512)} %param.6) | copy-start | bytes 4612
  16.8 9.5 %copy-start.2 = (s32[1,16]{1,0:T(1,128)S(1)}, s32[1,16]{1,0:T(1,128)}, u32[]{:S(2)}) copy-start(s32[1,16]{1,0:T(1,128)} %param.8) | copy-start | bytes 196
  16.8 500.9 %all-to-all-start = ((bf16[16,384,2048]{2,1,0:T(8,128)(2,1)}), bf16[16,384,2048]{2,1,0:T(8,128)(2,1)}, u32[]{:S(2)}, u32[]{:S(2)}) async-start(bf16[16,384,2048]{2,1,0:T(8,128)(2,1)} %stack.8), calls=%async_computation | async-start | bytes 50331648 | tf_op jit(solution)/shard_map/all_to_all | solution.py:14
  25.5 565.2 %reduce-scatter.2.cloned.1.call-start = ((), (), s32[]{:S(2)}) async-start(), calls=%async_computation.2 | async-start | bytes 7077888 | tf_op jit(solution)/shard_map/reduce_scatter | solution.py:64
  543.1 103.4 %all-gather.4.cloned.1.call-start = ((), (), s32[]{:S(2)}) async-start(), calls=%async_computation.3 | async-start | bytes 3538944 | tf_op jit(solution)/shard_map/all_gather | solution.py:76
  668.3 34.5 %copy-start.1 = (f32[384]{0:T(512)S(1)}, f32[384]{0:T(512)}, u32[]{:S(2)}) copy-start(f32[384]{0:T(512)} %param.6) | copy-start | bytes 4612
Sparse Core Ops, SparseCore 0:
  543.2 47.5 reduce-scatter.1
  615.4 30.9 all-gather.3
